TPU v7x, 32 devices: a whole 2x2x4 slice. The times are simulated.
32 devices in a mesh: row: 8 (over y, x, core), grp: 4 (over z).
Axes of the slice: x: 2, y: 2, z: 4, core: 2. Of those that a mesh axis runs over, the one named last changes fastest.
Arguments:
- positions: float32 [3, 1024], replicated, may hold values from -0.05 to 9.35, as said below
- detuning: float32 [1024], replicated, may hold values from -1 to 1
- populations: float32 [1024], P('row'), may hold values from 0 to 1
- base: float32 [2, 64, 1024], P(None, 'grp', 'row'), may hold values from -6 to 6
- section: float32 [2, 64, 1024], P(None, 'grp', 'row'), may hold values from -6 to 6
- accum: float32 [2, 64, 1024], P(None, 'grp', 'row'), may hold values from -3 to 3
Outputs:
- next_input: float32 [2, 64, 1024], P(None, 'grp', 'row')
- accum_out: float32 [2, 64, 1024], P(None, 'grp', 'row')
Inputs may be any that keep to these rules, and one draw needn't show every extreme that they name: `positions`: emitter n sits near the lattice point 0.3 * (n % 32, (n // 32) % 32, n // 1024), displaced by at most 0.05 in each coordinate.
All inputs are finite; a program needn't handle non-finite values.
Results may differ from a plain program's by a relative error of at most 0.0003.
Values sent between devices are 32-bit elements; how exact they have to be, the bound alone decides.
A program may use at most 64 MiB of HBM per device.

v0:
```python
import functools
import math

import jax
import jax.numpy as jnp
from jax import lax
from jax.experimental import pallas as pl
from jax.experimental.pallas import tpu as pltpu
from jax.sharding import PartitionSpec as P

TIME_STEP = 0.2
CHUNK = 32
PAD = 16

SIN_COEFFS = (
    6.283185302511502,
    -41.3417004053172,
    81.60513138578366,
    -76.7030153536576,
    42.02592698454004,
    -14.89984666366821,
    3.2381375046186873,
)
COS_COEFFS = (
    0.9999999890590228,
    -19.739204499453827,
    64.9391174598908,
    -85.45013953079768,
    60.16763095026347,
    -25.967599245923736,
    6.52865815775625,
)


def horner(coeffs, t):
    total = coeffs[-1] * t + coeffs[-2]
    for value in coeffs[-3::-1]:
        total = total * t + value
    return total


def coupling(cols, rows, diag):
    dx = cols[0] - rows[0]
    dy = cols[1] - rows[1]
    dz = cols[2] - rows[2]
    dz_sq = dz * dz
    dist_sq = dx * dx + dy * dy + dz_sq
    if diag is not None:
        dist_sq = jnp.where(diag, 1.0, dist_sq)
    inv = lax.rsqrt(dist_sq)
    dist = dist_sq * inv
    frac = dist - jnp.round(dist)
    t = frac * frac
    sine = frac * horner(SIN_COEFFS, t)
    cosine = horner(COS_COEFFS, t)
    aligned = dz_sq * (inv * inv)
    mix = 1.0 - 3.0 * aligned
    u = inv * (0.5 / math.pi)
    quad_imag = u * mix
    quad_real = (1.0 - aligned) - u * quad_imag
    scale = -0.75 * u
    amp_real = scale * quad_real
    amp_imag = scale * quad_imag
    h_real = amp_real * cosine - amp_imag * sine
    h_imag = amp_real * sine + amp_imag * cosine
    if diag is not None:
        h_real = jnp.where(diag, 0.0, h_real)
        h_imag = jnp.where(diag, 0.0, h_imag)
    return h_real, h_imag


def split(x):
    hi = x.astype(jnp.bfloat16)
    return hi, (x - hi.astype(jnp.float32)).astype(jnp.bfloat16)


def bdot(a, b):
    return jnp.dot(a, b, preferred_element_type=jnp.float32)


def kernel(
    n_row,
    n_grp,
    pos_in,
    det_in,
    pop_in,
    sec_in,
    out_ref,
    pos_ref,
    det_ref,
    stage,
    pos_t,
    rhs_hi,
    rhs_lo,
    row_buf,
    grp_buf,
    sec_send,
    sec_recv,
    grp_send,
    grp_recv,
    load_sem,
):
    cols, width = sec_in.shape[1], sec_in.shape[2]
    loads = []
    for i, (src, dst) in enumerate(
        (
            (sec_in.at[0], stage.at[0:cols]),
            (sec_in.at[1], stage.at[cols : 2 * cols]),
            (pop_in, stage.at[2 * cols : 2 * cols + 1]),
            (pos_in, pos_ref),
            (det_in, det_ref),
        )
    ):
        load = pltpu.make_async_copy(src, dst, load_sem.at[i])
        load.start()
        loads.append(load)
    me = lax.axis_index("row")
    mine = lax.axis_index("grp")
    slab = cols * n_grp

    def row_peer(s):
        return lax.rem(me + s, n_row)

    def grp_peer(s):
        return lax.rem(mine + s, n_grp)

    barrier = pltpu.get_barrier_semaphore()
    for s in range(1, n_row):
        pl.semaphore_signal(barrier, inc=1, device_id={"row": row_peer(s)}, device_id_type=pl.DeviceIdType.MESH)
    for s in range(1, n_grp):
        pl.semaphore_signal(barrier, inc=1, device_id={"grp": grp_peer(s)}, device_id_type=pl.DeviceIdType.MESH)

    loads[0].wait()
    loads[1].wait()
    pl.semaphore_wait(barrier, n_row + n_grp - 2)

    loads[2].wait()
    row_copies = {}
    for s in range(1, n_row):
        copy = pltpu.make_async_remote_copy(
            stage,
            row_buf.at[s],
            sec_send.at[s],
            sec_recv.at[s],
            device_id={"row": row_peer(s)},
            device_id_type=pl.DeviceIdType.MESH,
        )
        copy.start()
        row_copies[s] = copy
    slab_part = stage.at[0 : 2 * cols]
    grp_copies = []
    for s in range(1, n_grp):
        copy = pltpu.make_async_remote_copy(
            slab_part,
            grp_buf.at[s],
            grp_send.at[s],
            grp_recv.at[s],
            device_id={"grp": grp_peer(s)},
            device_id_type=pl.DeviceIdType.MESH,
        )
        copy.start()
        grp_copies.append(copy)

    loads[3].wait()
    loads[4].wait()
    for b in range(n_row):
        part = pos_ref[:, b * width : (b + 1) * width]
        tall = jnp.concatenate([part, jnp.zeros((5, width), jnp.float32)], axis=0)
        pos_t[b * width : (b + 1) * width, :] = jnp.transpose(tall)

    my_start = pl.multiple_of(me * width, width)
    rows = [pos_ref[d : d + 1, pl.ds(my_start, width)] for d in range(3)]
    chunks = width // CHUNK

    def fill(slot_row, pos_row, diag):
        block = pos_t[pl.ds(pos_row, CHUNK), :]
        h_real, h_imag = coupling([block[:, d : d + 1] for d in range(3)], rows, diag)
        for lane, h in ((0, h_real), (width, h_imag)):
            hi, lo = split(h)
            rhs_hi[pl.ds(slot_row, CHUNK), lane : lane + width] = hi
            rhs_lo[pl.ds(slot_row, CHUNK), lane : lane + width] = lo

    lane_ids = lax.broadcasted_iota(jnp.int32, (CHUNK, width), 1)
    sub_ids = lax.broadcasted_iota(jnp.int32, (CHUNK, width), 0)

    def own_chunk(j, carry):
        offset = pl.multiple_of(j * CHUNK, CHUNK)
        fill(offset, pl.multiple_of(my_start + offset, CHUNK), sub_ids + offset == lane_ids)
        return carry

    def other_chunk(j, carry):
        offset = pl.multiple_of(j * CHUNK, CHUNK)
        owner = lax.rem(me + n_row - j // chunks, n_row)
        start = owner * width + lax.rem(j, chunks) * CHUNK
        fill(offset, pl.multiple_of(start, CHUNK), None)
        return carry

    lax.fori_loop(0, chunks, own_chunk, 0)

    col_start = pl.multiple_of(mine * cols, cols)
    own_pos = pos_t[pl.ds(col_start, cols), :]
    own_cols = [own_pos[:, d : d + 1] for d in range(3)]
    slab_diag = lax.broadcasted_iota(jnp.int32, (cols, width), 0) + col_start == lax.broadcasted_iota(
        jnp.int32, (cols, width), 1
    )
    slab_rows = [pos_ref[d : d + 1, :width] for d in range(3)]
    w_real, w_imag = coupling(own_cols, slab_rows, slab_diag)
    w_real = w_real + jnp.where(slab_diag, det_ref[:, :width], 0.0)
    w_imag = w_imag + jnp.where(slab_diag, -0.5, 0.0)
    lead_all = jnp.concatenate([w_real, w_imag], axis=0)

    lax.fori_loop(chunks, n_row * chunks, other_chunk, 0, unroll=2)

    def left(slab_and_pop):
        signed = jnp.broadcast_to(2.0 * slab_and_pop[2 * cols :] - 1.0, (PAD, width))
        return split(jnp.concatenate([slab_and_pop[: 2 * cols], signed], axis=0))

    y_local = stage[0 : 2 * cols]
    main = jnp.zeros((4 * cols + 2 * PAD, 2 * width), jnp.float32)
    rest = jnp.zeros((2 * cols + PAD, 2 * width), jnp.float32)
    group = 2 if n_row % 2 == 0 else 1
    for first in range(0, n_row, group):
        his, los = [], []
        for s in range(first, first + group):
            if s == 0:
                hi, lo = left(stage[...])
            else:
                row_copies[s].wait_recv()
                hi, lo = left(row_buf[s])
            his.append(hi)
            los.append(lo)
        hi = jnp.concatenate(his, axis=1)
        lo = jnp.concatenate(los, axis=1)
        span = slice(first * width, (first + group) * width)
        main = main + bdot(jnp.concatenate([hi, lo], axis=0), rhs_hi[span, :])
        rest = rest + bdot(hi, rhs_lo[span, :])
    half = 2 * cols + PAD
    z = main[:half] + main[half:] + rest
    z_real = z[:cols, :width] - z[cols : 2 * cols, width:]
    z_imag = z[:cols, width:] + z[cols : 2 * cols, :width]
    shift = z[2 * cols : 2 * cols + 1, :width]

    for copy in grp_copies:
        copy.wait_recv()
    grp_buf[0] = y_local
    blocks = [grp_buf[lax.rem(mine + n_grp - g, n_grp)] for g in range(n_grp)]
    full = jnp.concatenate(
        [jnp.concatenate([block[:cols], block[cols:]], axis=1) for block in blocks], axis=0
    )
    f_hi, f_lo = split(full)
    l_hi, l_lo = split(lead_all[:, :slab])
    v = bdot(l_hi, f_hi) + bdot(l_lo, f_hi) + bdot(l_hi, f_lo)
    v_real = v[:cols, :width] + v[cols:, width:]
    v_imag = v[:cols, width:] - v[cols:, :width]

    y_real, y_imag = y_local[:cols], y_local[cols:]
    total_shift = shift + det_ref[:, pl.ds(my_start, width)]
    z_real = z_real + total_shift * y_real + 0.5 * y_imag
    z_imag = z_imag + total_shift * y_imag - 0.5 * y_real
    out_ref[0] = z_imag - v_imag
    out_ref[1] = v_real - z_real

    for copy in list(row_copies.values()) + grp_copies:
        copy.wait_send()


def local(positions, detuning, populations, base, section, accum):
    n_row, n_grp = lax.axis_size("row"), lax.axis_size("grp")
    cols, width = section.shape[1], section.shape[2]
    total = positions.shape[1]
    block = section.shape
    rate = pl.pallas_call(
        functools.partial(kernel, n_row, n_grp),
        out_shape=pltpu.VMEM(block, jnp.float32),
        in_specs=[pl.BlockSpec(memory_space=pl.ANY)] * 4,
        out_specs=pl.BlockSpec(memory_space=pltpu.VMEM),
        scratch_shapes=[
            pltpu.VMEM((3, total), jnp.float32),
            pltpu.VMEM((1, total), jnp.float32),
            pltpu.VMEM((2 * cols + 1, width), jnp.float32),
            pltpu.VMEM((total, 8), jnp.float32),
            pltpu.VMEM((total, 2 * width), jnp.bfloat16),
            pltpu.VMEM((total, 2 * width), jnp.bfloat16),
            pltpu.VMEM((n_row, 2 * cols + 1, width), jnp.float32),
            pltpu.VMEM((n_grp, 2 * cols, width), jnp.float32),
            pltpu.SemaphoreType.DMA((n_row,)),
            pltpu.SemaphoreType.DMA((n_row,)),
            pltpu.SemaphoreType.DMA((n_grp,)),
            pltpu.SemaphoreType.DMA((n_grp,)),
            pltpu.SemaphoreType.DMA((5,)),
        ],
        compiler_params=pltpu.CompilerParams(collective_id=0, has_side_effects=True),
    )(positions, detuning.reshape(1, total), populations.reshape(1, width), section)
    return (base + 0.5 * TIME_STEP * rate, accum + TIME_STEP / 3.0 * rate)


def solution(mesh):
    return jax.shard_map(
        local,
        mesh=mesh,
        in_specs=(
            P(),
            P(),
            P("row"),
            P(None, "grp", "row"),
            P(None, "grp", "row"),
            P(None, "grp", "row"),
        ),
        out_specs=(P(None, "grp", "row"), P(None, "grp", "row")),
        check_vma=False,
    )
```

profile of v0, /device:TPU:0, one launch (start us, length us, event | category | flops | bytes accessed | tf_op | source)
XLA Modules:
  0.0 11.8 jit_solution(3427077061657421365)
XLA Ops:
  0.6 0.0 copy-start
  0.6 0.0 copy-start.1
  0.7 10.5 %shard_map.77 = f32[2,16,128]{2,1,0:T(8,128)S(1)} custom-call(f32[3,1024]{1,0:T(4,128)} %pos_in.1, f32[1,1024]{1,0:T(1,128)} %bitcast.2, f32[1,128]{1,0:T(1,128)} %bitcast.3, f32[2,16,128]{2,1,0:T(8,128)} %sec_in.1), custom_call_target="tpu_custom_call" | custom-call | tf_op jit(solution)/shard_map/pallas_call | solution.py:272
  11.1 0.0 copy-done
  11.1 0.0 copy-done.1
  11.1 0.6 %multiply_add_fusion = (f32[2,16,128]{2,1,0:T(8,128)}, f32[2,16,128]{2,1,0:T(8,128)}) fusion(f32[2,16,128]{2,1,0:T(8,128)S(1)} %copy-done, f32[2,16,128]{2,1,0:T(8,128)S(1)} %shard_map.77, f32[2,16,128]{2,1,0:T(8,128)S(1)} %copy-done.1), kind=kLoop, calls=%fused_computation | loop fusion | flops 16384 | bytes 81920 | tf_op jit(solution)/shard_map/add | solution.py:294
Async XLA Ops:
  0.6 10.5 %copy-start = (f32[2,16,128]{2,1,0:T(8,128)S(1)}, f32[2,16,128]{2,1,0:T(8,128)}, u32[]{:S(2)}) copy-start(f32[2,16,128]{2,1,0:T(8,128)} %param.11) | copy-start | bytes 49156
  0.6 10.5 %copy-start.1 = (f32[2,16,128]{2,1,0:T(8,128)S(1)}, f32[2,16,128]{2,1,0:T(8,128)}, u32[]{:S(2)}) copy-start(f32[2,16,128]{2,1,0:T(8,128)} %param.9) | copy-start | bytes 49156
where the time goes:
time: 11.9 us; the launch traced here: 11.8 us
  Pallas kernels  10.5 us (88%)
  between operations  0.67 us (6%)
  other arithmetic  0.62 us (5%)
    pallas_call x1, Pallas kernels, local(): pl.pallas_call(functools.partial(kernel, n_row, n_grp), out_shape=pltpu.V...  10.5 us
    add x1, other arithmetic, local(): return (base + 0.5 * TIME_STEP * rate, accum + TIME_STEP / 3.0 * rate)  0.62 us

commit v1 on v0

v1 whole, which is shorter than its diff:
```python
import functools
import math

import jax
import jax.numpy as jnp
from jax import lax
from jax.experimental import pallas as pl
from jax.experimental.pallas import tpu as pltpu
from jax.sharding import PartitionSpec as P

TIME_STEP = 0.2
PAD = 16
TILE = 128
AMPLITUDE = -0.75

HALF_SIN = (4.442882834149929, -7.308241154546326, 3.606288958225646, -0.8457635961475002, 0.10920575363724722)
HALF_COS = (1.4142134965650124, -6.97885098823893, 5.739461170681154, -1.8835629872981716, 0.31069819180355424)
MESH = pl.DeviceIdType.MESH


def horner(coeffs, t):
    total = coeffs[-1] * t + coeffs[-2]
    for value in coeffs[-3::-1]:
        total = total * t + value
    return total


def coupling(cols, rows, diag):
    dx = cols[0] - rows[0]
    dy = cols[1] - rows[1]
    dz = cols[2] - rows[2]
    dz_sq = dz * dz
    dist_sq = dx * dx + dy * dy + dz_sq
    if diag is not None:
        dist_sq = jnp.where(diag, 1.0, dist_sq)
    inv = lax.rsqrt(dist_sq)
    dist = dist_sq * inv
    frac = dist - jnp.round(dist)
    t = frac * frac
    half_sin = frac * horner(HALF_SIN, t)
    half_cos = horner(HALF_COS, t)
    sine = half_sin * half_cos
    cosine = 1.0 - half_sin * half_sin
    u = inv * (0.5 / math.pi)
    aligned = dz_sq * (inv * inv)
    amp_imag = (u * u) * (1.0 - 3.0 * aligned)
    amp_real = u * ((1.0 - aligned) - amp_imag)
    h_real = amp_real * cosine - amp_imag * sine
    h_imag = amp_real * sine + amp_imag * cosine
    if diag is not None:
        h_real = jnp.where(diag, 0.0, h_real)
        h_imag = jnp.where(diag, 0.0, h_imag)
    return h_real, h_imag


def split(x):
    hi = x.astype(jnp.bfloat16)
    return hi, (x - hi.astype(jnp.float32)).astype(jnp.bfloat16)


def bdot(a, b):
    return jnp.dot(a, b, preferred_element_type=jnp.float32)


def kernel(
    n_row,
    n_grp,
    pos_in,
    det_in,
    pop_in,
    sec_in,
    out_ref,
    pos_ref,
    det_ref,
    stage,
    wide,
    rhs_hi,
    rhs_lo,
    row_buf,
    grp_buf,
    send_sem,
    row_recv,
    grp_recv,
    row_ready,
    grp_ready,
    load_sem,
):
    cols, width = sec_in.shape[1], sec_in.shape[2]
    section_loads = [
        pltpu.make_async_copy(src, dst, load_sem.at[0])
        for src, dst in (
            (sec_in.at[0], stage.at[0:cols]),
            (sec_in.at[1], stage.at[cols : 2 * cols]),
            (pop_in, stage.at[2 * cols : 2 * cols + 1]),
        )
    ]
    pos_load = pltpu.make_async_copy(pos_in, pos_ref, load_sem.at[1])
    det_load = pltpu.make_async_copy(det_in, det_ref, load_sem.at[2])
    for load in (*section_loads, pos_load, det_load):
        load.start()
    me = lax.axis_index("row")
    mine = lax.axis_index("grp")
    slab = cols * n_grp

    barrier = pltpu.get_barrier_semaphore()

    last = n_row - 2
    pair = me // 2
    odd = lax.rem(me, 2)
    partner = me + 1 - 2 * odd
    in_first = me < 2
    in_last = me >= last
    between = jnp.logical_not(in_first | in_last)
    GO, LATE = 0, 1

    def to_row(sem, lo, hi):
        def body(p, carry):
            pl.semaphore_signal(sem, inc=1, device_id={"row": p}, device_id_type=MESH)
            return carry

        lax.fori_loop(lo, hi, body, 0)

    def to_grp(sem, lo, hi):
        def body(p, carry):
            pl.semaphore_signal(sem, inc=1, device_id={"grp": p}, device_id_type=MESH)
            return carry

        lax.fori_loop(lo, hi, body, 0)

    slab_part = stage.at[0 : 2 * cols]

    def send_row(lo, hi):
        def body(p, carry):
            pltpu.make_async_remote_copy(
                stage,
                row_buf.at[me],
                send_sem.at[0],
                row_recv.at[pair],
                device_id={"row": p},
                device_id_type=MESH,
            ).start()
            return carry

        lax.fori_loop(lo, hi, body, 0)

    def send_grp(lo, hi):
        def body(p, carry):
            pltpu.make_async_remote_copy(
                slab_part,
                grp_buf.at[mine],
                send_sem.at[1],
                grp_recv,
                device_id={"grp": p},
                device_id_type=MESH,
            ).start()
            return carry

        lax.fori_loop(lo, hi, body, 0)

    def arrived(part, sem):
        pltpu.make_async_copy(part, part, sem).wait()

    to_grp(barrier, mine + 1, n_grp)

    @pl.when(odd == 1)
    def _():
        pl.semaphore_signal(barrier, inc=1, device_id={"row": partner}, device_id_type=MESH)

    after = jnp.where(in_first, 2, jnp.where(in_last, n_row, last))
    to_row(barrier, after, n_row)

    before = jnp.where(in_first, 0, jnp.where(in_last, last, 2))
    met = before + (1 - odd) + mine

    @pl.when(met > 0)
    def _():
        with jax.named_scope("bar"):
            pl.semaphore_wait(barrier, met)

    to_grp(grp_ready.at[mine], 0, mine)

    @pl.when(between)
    def _():
        to_row(row_ready.at[GO], 0, 2)

    @pl.when(in_last)
    def _():
        to_row(row_ready.at[LATE], 0, last)

    @pl.when(odd == 0)
    def _():
        pl.semaphore_signal(row_ready.at[LATE], inc=1, device_id={"row": partner}, device_id_type=MESH)

    with jax.named_scope("load"):
        arrived(stage, load_sem.at[0])
    send_grp(0, mine)
    send_row(0, before)

    @pl.when(odd == 0)
    def _():
        send_row(partner, partner + 1)

    with jax.named_scope("loadpos"):
        pos_load.wait()
        det_load.wait()

    my_start = pl.multiple_of(me * width, width)
    rows = [pos_ref[d : d + 1, pl.ds(my_start, width)] for d in range(3)]
    tiles = width // TILE

    def spread(tile, slot):
        start = pl.multiple_of(tile * TILE, TILE)
        for d in range(3):
            line = pos_ref[d : d + 1, pl.ds(start, TILE)]
            wide[slot, d] = jnp.transpose(jnp.broadcast_to(line, (TILE, TILE)))

    def fill(tile, slot, diag):
        start = pl.multiple_of(tile * TILE, TILE)
        for part in range(tiles):
            lanes = slice(part * TILE, (part + 1) * TILE)
            h_real, h_imag = coupling(
                [wide[slot, d] for d in range(3)],
                [r[:, lanes] for r in rows],
                None if diag is None else diag[:, lanes],
            )
            for base, h in ((0, h_real), (width, h_imag)):
                hi, lo = split(h)
                at = slice(base + part * TILE, base + (part + 1) * TILE)
                rhs_hi[pl.ds(start, TILE), at] = hi
                rhs_lo[pl.ds(start, TILE), at] = lo

    first = me * tiles
    total = n_row * tiles
    lane_ids = lax.broadcasted_iota(jnp.int32, (TILE, width), 1)
    sub_ids = lax.broadcasted_iota(jnp.int32, (TILE, width), 0)

    def tile_at(j):
        return lax.rem(first + j, total)

    with jax.named_scope("couple"):
        spread(first, 0)
        for j in range(tiles):
            spread(tile_at(j + 1), (j + 1) % 2)
            fill(tile_at(j), j % 2, sub_ids + j * TILE == lane_ids)

        def step(j, carry):
            spread(tile_at(j + 1), lax.rem(j + 1, 2))
            fill(tile_at(j), lax.rem(j, 2), None)
            return carry

        UNROLL = 7 if (total - tiles) % 7 == 0 else 1
        if UNROLL == total - tiles:
            for j in range(tiles, total):
                if j + 1 < total:
                    spread(tile_at(j + 1), (j + 1) % 2)
                fill(tile_at(j), j % 2, None)
        else:
            lax.fori_loop(tiles, total, step, 0)

    def answer_grp(p, carry):
        pl.semaphore_wait(grp_ready.at[p], 1)
        send_grp(p, p + 1)
        return carry

    @pl.when(in_first & (last > 2))
    def _():
        with jax.named_scope("wmid"):
            pl.semaphore_wait(row_ready.at[GO], last - 2)

        @pl.when(odd == 1)
        def _():
            to_row(row_ready.at[GO], 2, last)

        send_row(2, last)

    @pl.when(between)
    def _():
        with jax.named_scope("wgo"):
            pl.semaphore_wait(row_ready.at[GO], 1)
        send_row(2, 2 * pair)
        send_row(2 * pair + 2, last)

    with jax.named_scope("ansgrp1"):
        lax.fori_loop(mine + 1, jnp.minimum(mine + 2, n_grp), answer_grp, 0)
    late = odd + jnp.where(in_last, 0, 2)

    @pl.when(late > 0)
    def _():
        with jax.named_scope("wlate"):
            pl.semaphore_wait(row_ready.at[LATE], late)

    @pl.when(odd == 1)
    def _():
        send_row(partner, partner + 1)

    @pl.when(jnp.logical_not(in_last))
    def _():
        send_row(last, n_row)

    with jax.named_scope("ansgrp2"):
        lax.fori_loop(mine + 2, n_grp, answer_grp, 0)

    col_start = pl.multiple_of(mine * cols, cols)
    eye = lax.broadcasted_iota(jnp.int32, (cols, TILE), 0) + col_start == lax.broadcasted_iota(
        jnp.int32, (cols, TILE), 1
    )
    slab_rows = [pos_ref[d : d + 1, :TILE] for d in range(3)]
    own_cols = [
        jnp.sum(jnp.where(eye, jnp.broadcast_to(r, (cols, TILE)), 0.0), axis=1, keepdims=True) for r in slab_rows
    ]
    w_real, w_imag = coupling(own_cols, slab_rows, eye)
    w_real = AMPLITUDE * w_real + jnp.where(eye, det_ref[:, :TILE], 0.0)
    w_imag = AMPLITUDE * w_imag + jnp.where(eye, -0.5, 0.0)
    l_hi, l_lo = split(jnp.concatenate([w_real, w_imag], axis=0)[:, :slab])

    y_local = stage[0 : 2 * cols]
    row_buf[me] = stage[...]
    grp_buf[mine] = y_local

    def left(slab_and_pop):
        signed = jnp.broadcast_to(2.0 * slab_and_pop[2 * cols :] - 1.0, (PAD, width))
        return split(jnp.concatenate([slab_and_pop[: 2 * cols], signed], axis=0))

    main = jnp.zeros((4 * cols + 2 * PAD, 2 * width), jnp.float32)
    rest = jnp.zeros((2 * cols + PAD, 2 * width), jnp.float32)
    group = 2
    for lead in range(0, n_row, group):
        his, los = [], []
        with jax.named_scope(f"wrow{lead}"):

            @pl.when(pair == lead // 2)
            def _():
                arrived(row_buf.at[0], row_recv.at[lead // 2])

            @pl.when(pair != lead // 2)
            def _():
                arrived(row_buf.at[0:2], row_recv.at[lead // 2])

        for p in range(lead, lead + group):
            hi, lo = left(row_buf[p])
            his.append(hi)
            los.append(lo)
        hi = jnp.concatenate(his, axis=1)
        lo = jnp.concatenate(los, axis=1)
        span = slice(lead * width, (lead + group) * width)
        main = main + bdot(jnp.concatenate([hi, lo], axis=0), rhs_hi[span, :])
        rest = rest + bdot(hi, rhs_lo[span, :])
    half = 2 * cols + PAD
    z = AMPLITUDE * (main[:half] + main[half:] + rest)
    z_real = z[:cols, :width] - z[cols : 2 * cols, width:]
    z_imag = z[:cols, width:] + z[cols : 2 * cols, :width]
    shift = z[2 * cols : 2 * cols + 1, :width]

    with jax.named_scope("wgrp"):
        arrived(grp_buf.at[0 : n_grp - 1], grp_recv)
    blocks = [grp_buf[g] for g in range(n_grp)]
    full = jnp.concatenate(
        [jnp.concatenate([block[:cols], block[cols:]], axis=1) for block in blocks], axis=0
    )
    f_hi, f_lo = split(full)
    v = bdot(l_hi, f_hi) + bdot(l_lo, f_hi) + bdot(l_hi, f_lo)
    v_real = v[:cols, :width] + v[cols:, width:]
    v_imag = v[:cols, width:] - v[cols:, :width]

    y_real, y_imag = y_local[:cols], y_local[cols:]
    total_shift = shift + det_ref[:, pl.ds(my_start, width)]
    z_real = z_real + total_shift * y_real + 0.5 * y_imag
    z_imag = z_imag + total_shift * y_imag - 0.5 * y_real
    out_ref[0] = z_imag - v_imag
    out_ref[1] = v_real - z_real

    with jax.named_scope("drain"):
        arrived(row_buf.at[0 : n_row - 1], send_sem.at[0])
        arrived(grp_buf.at[0 : n_grp - 1], send_sem.at[1])


def local(positions, detuning, populations, base, section, accum):
    n_row, n_grp = lax.axis_size("row"), lax.axis_size("grp")
    cols, width = section.shape[1], section.shape[2]
    total = positions.shape[1]
    block = section.shape
    rate = pl.pallas_call(
        functools.partial(kernel, n_row, n_grp),
        out_shape=pltpu.VMEM(block, jnp.float32),
        in_specs=[pl.BlockSpec(memory_space=pl.ANY)] * 4,
        out_specs=pl.BlockSpec(memory_space=pltpu.VMEM),
        scratch_shapes=[
            pltpu.VMEM((3, total), jnp.float32),
            pltpu.VMEM((1, total), jnp.float32),
            pltpu.VMEM((2 * cols + 1, width), jnp.float32),
            pltpu.VMEM((2, 3, TILE, TILE), jnp.float32),
            pltpu.VMEM((total, 2 * width), jnp.bfloat16),
            pltpu.VMEM((total, 2 * width), jnp.bfloat16),
            pltpu.VMEM((n_row, 2 * cols + 1, width), jnp.float32),
            pltpu.VMEM((n_grp, 2 * cols, width), jnp.float32),
            pltpu.SemaphoreType.DMA((2,)),
            pltpu.SemaphoreType.DMA((n_row // 2,)),
            pltpu.SemaphoreType.DMA(()),
            pltpu.SemaphoreType.REGULAR((2,)),
            pltpu.SemaphoreType.REGULAR((n_grp,)),
            pltpu.SemaphoreType.DMA((3,)),
        ],
        compiler_params=pltpu.CompilerParams(collective_id=0, has_side_effects=True),
    )(positions, detuning.reshape(1, total), populations.reshape(1, width), section)
    return (base + 0.5 * TIME_STEP * rate, accum + TIME_STEP / 3.0 * rate)


def solution(mesh):
    return jax.shard_map(
        local,
        mesh=mesh,
        in_specs=(
            P(),
            P(),
            P("row"),
            P(None, "grp", "row"),
            P(None, "grp", "row"),
            P(None, "grp", "row"),
        ),
        out_specs=(P(None, "grp", "row"), P(None, "grp", "row")),
        check_vma=False,
    )
```

time: 11.9 us -> 9.28 us (0.78)
  Pallas kernels: 10.5 us -> 7.81 us
    pallas_call x1, Pallas kernels: 10.5 us -> 7.81 us  [local(): pl.pallas_call(functools.partial(kernel, n_row, n_grp), out_shape=pltpu.V...]
where the time goes in v1:
time: 9.28 us; the launch traced here: 9.1 us
  Pallas kernels  7.81 us (84%)
  between operations  0.67 us (7%)
  other arithmetic  0.62 us (7%)
    pallas_call x1, Pallas kernels, local(): pl.pallas_call(functools.partial(kernel, n_row, n_grp), out_shape=pltpu.V...  7.81 us
    add x1, other arithmetic, local(): return (base + 0.5 * TIME_STEP * rate, accum + TIME_STEP / 3.0 * rate)  0.62 us

profile of v1, /device:TPU:0, one launch (start us, length us, event | category | flops | bytes accessed | tf_op | source)
XLA Modules:
  0.0 9.1 jit_solution(7387423909517939459)
XLA Ops:
  0.6 0.0 copy-start
  0.6 0.0 copy-start.1
  0.7 7.8 %shard_map.77 = f32[2,16,128]{2,1,0:T(8,128)S(1)} custom-call(f32[3,1024]{1,0:T(4,128)} %pos_in.1, f32[1,1024]{1,0:T(1,128)} %bitcast.2, f32[1,128]{1,0:T(1,128)} %bitcast.3, f32[2,16,128]{2,1,0:T(8,128)} %sec_in.1), custom_call_target="tpu_custom_call" | custom-call | tf_op jit(solution)/shard_map/pallas_call | solution.py:382
  8.5 0.0 copy-done
  8.5 0.0 copy-done.1
  8.5 0.6 %multiply_add_fusion = (f32[2,16,128]{2,1,0:T(8,128)}, f32[2,16,128]{2,1,0:T(8,128)}) fusion(f32[2,16,128]{2,1,0:T(8,128)S(1)} %copy-done, f32[2,16,128]{2,1,0:T(8,128)S(1)} %shard_map.77, f32[2,16,128]{2,1,0:T(8,128)S(1)} %copy-done.1), kind=kLoop, calls=%fused_computation | loop fusion | flops 16384 | bytes 81920 | tf_op jit(solution)/shard_map/add | solution.py:405
Async XLA Ops:
  0.6 7.8 %copy-start = (f32[2,16,128]{2,1,0:T(8,128)S(1)}, f32[2,16,128]{2,1,0:T(8,128)}, u32[]{:S(2)}) copy-start(f32[2,16,128]{2,1,0:T(8,128)} %param.11) | copy-start | bytes 49156
  0.6 7.8 %copy-start.1 = (f32[2,16,128]{2,1,0:T(8,128)S(1)}, f32[2,16,128]{2,1,0:T(8,128)}, u32[]{:S(2)}) copy-start(f32[2,16,128]{2,1,0:T(8,128)} %param.9) | copy-start | bytes 49156

commit v2 on v1

--- a/solution.py
+++ b/solution.py
@@ -85,12 +85,11 @@
     grp_ready,
     load_sem,
 ):
-    cols, width = sec_in.shape[1], sec_in.shape[2]
+    cols, width = sec_in.shape[0] // 2, sec_in.shape[1]
     section_loads = [
         pltpu.make_async_copy(src, dst, load_sem.at[0])
         for src, dst in (
-            (sec_in.at[0], stage.at[0:cols]),
-            (sec_in.at[1], stage.at[cols : 2 * cols]),
+            (sec_in, stage.at[0 : 2 * cols]),
             (pop_in, stage.at[2 * cols : 2 * cols + 1]),
         )
     ]
@@ -111,7 +110,8 @@
     in_first = me < 2
     in_last = me >= last
     between = jnp.logical_not(in_first | in_last)
-    GO, LATE = 0, 1
+    even = odd == 0
+    GO, LATE, WORD = 0, 1, 2
 
     def to_row(sem, lo, hi):
         def body(p, carry):
@@ -135,7 +135,7 @@
                 stage,
                 row_buf.at[me],
                 send_sem.at[0],
-                row_recv.at[pair],
+                row_recv.at[me // last],
                 device_id={"row": p},
                 device_id_type=MESH,
             ).start()
@@ -143,10 +143,10 @@
 
         lax.fori_loop(lo, hi, body, 0)
 
-    def send_grp(lo, hi):
+    def send_grp(lo, hi, source):
         def body(p, carry):
             pltpu.make_async_remote_copy(
-                slab_part,
+                source,
                 grp_buf.at[mine],
                 send_sem.at[1],
                 grp_recv,
@@ -160,9 +160,19 @@
     def arrived(part, sem):
         pltpu.make_async_copy(part, part, sem).wait()
 
-    to_grp(barrier, mine + 1, n_grp)
-
-    @pl.when(odd == 1)
+    @pl.when(even & (mine > 0))
+    def _():
+        def body(p, carry):
+            pl.semaphore_signal(barrier, inc=1, device_id={"row": partner, "grp": p}, device_id_type=MESH)
+            return carry
+
+        lax.fori_loop(mine + 1, n_grp, body, 0)
+
+    @pl.when(jnp.logical_not(even & (mine > 0)))
+    def _():
+        to_grp(barrier, mine + 1, n_grp)
+
+    @pl.when(even)
     def _():
         pl.semaphore_signal(barrier, inc=1, device_id={"row": partner}, device_id_type=MESH)
 
@@ -170,14 +180,16 @@
     to_row(barrier, after, n_row)
 
     before = jnp.where(in_first, 0, jnp.where(in_last, last, 2))
-    met = before + (1 - odd) + mine
+    low = jnp.minimum(mine, 1)
+    met = before + jnp.where(even, low, 1 + mine + mine - low)
 
     @pl.when(met > 0)
     def _():
         with jax.named_scope("bar"):
             pl.semaphore_wait(barrier, met)
 
-    to_grp(grp_ready.at[mine], 0, mine)
+    send_grp(0, low, sec_in)
+    to_grp(grp_ready.at[mine - low], 0, low)
 
     @pl.when(between)
     def _():
@@ -187,18 +199,23 @@
     def _():
         to_row(row_ready.at[LATE], 0, last)
 
-    @pl.when(odd == 0)
-    def _():
-        pl.semaphore_signal(row_ready.at[LATE], inc=1, device_id={"row": partner}, device_id_type=MESH)
+    @pl.when(jnp.logical_not(even))
+    def _():
+        pl.semaphore_signal(row_ready.at[WORD], inc=1, device_id={"row": partner}, device_id_type=MESH)
+        to_grp(grp_ready.at[mine - low], low, mine)
 
     with jax.named_scope("load"):
         arrived(stage, load_sem.at[0])
-    send_grp(0, mine)
     send_row(0, before)
 
-    @pl.when(odd == 0)
-    def _():
-        send_row(partner, partner + 1)
+    @pl.when(even)
+    def _():
+        with jax.named_scope("word"):
+            pl.semaphore_wait(row_ready.at[WORD], 1)
+        to_grp(grp_ready.at[mine - low], low, mine)
+
+    send_grp(low, mine, slab_part)
+    send_row(partner, partner + 1)
 
     with jax.named_scope("loadpos"):
         pos_load.wait()
@@ -258,8 +275,8 @@
             lax.fori_loop(tiles, total, step, 0)
 
     def answer_grp(p, carry):
-        pl.semaphore_wait(grp_ready.at[p], 1)
-        send_grp(p, p + 1)
+        pl.semaphore_wait(grp_ready.at[p - 1], 1)
+        send_grp(p, p + 1, slab_part)
         return carry
 
     @pl.when(in_first & (last > 2))
@@ -282,19 +299,11 @@
 
     with jax.named_scope("ansgrp1"):
         lax.fori_loop(mine + 1, jnp.minimum(mine + 2, n_grp), answer_grp, 0)
-    late = odd + jnp.where(in_last, 0, 2)
-
-    @pl.when(late > 0)
+
+    @pl.when(jnp.logical_not(in_last))
     def _():
         with jax.named_scope("wlate"):
-            pl.semaphore_wait(row_ready.at[LATE], late)
-
-    @pl.when(odd == 1)
-    def _():
-        send_row(partner, partner + 1)
-
-    @pl.when(jnp.logical_not(in_last))
-    def _():
+            pl.semaphore_wait(row_ready.at[LATE], 2)
         send_row(last, n_row)
 
     with jax.named_scope("ansgrp2"):
@@ -326,15 +335,17 @@
     group = 2
     for lead in range(0, n_row, group):
         his, los = [], []
-        with jax.named_scope(f"wrow{lead}"):
-
-            @pl.when(pair == lead // 2)
-            def _():
-                arrived(row_buf.at[0], row_recv.at[lead // 2])
-
-            @pl.when(pair != lead // 2)
-            def _():
-                arrived(row_buf.at[0:2], row_recv.at[lead // 2])
+        for at, count in ((0, last), (last, 2)):
+            if lead == at:
+                with jax.named_scope(f"wrow{lead}"):
+
+                    @pl.when(in_last == (at == last))
+                    def _():
+                        arrived(row_buf.at[0 : count - 1], row_recv.at[at // last])
+
+                    @pl.when(in_last != (at == last))
+                    def _():
+                        arrived(row_buf.at[0:count], row_recv.at[at // last])
 
         for p in range(lead, lead + group):
             hi, lo = left(row_buf[p])
@@ -394,14 +405,14 @@
             pltpu.VMEM((n_row, 2 * cols + 1, width), jnp.float32),
             pltpu.VMEM((n_grp, 2 * cols, width), jnp.float32),
             pltpu.SemaphoreType.DMA((2,)),
-            pltpu.SemaphoreType.DMA((n_row // 2,)),
+            pltpu.SemaphoreType.DMA((2,)),
             pltpu.SemaphoreType.DMA(()),
-            pltpu.SemaphoreType.REGULAR((2,)),
-            pltpu.SemaphoreType.REGULAR((n_grp,)),
+            pltpu.SemaphoreType.REGULAR((3,)),
+            pltpu.SemaphoreType.REGULAR((n_grp - 1,)),
             pltpu.SemaphoreType.DMA((3,)),
         ],
         compiler_params=pltpu.CompilerParams(collective_id=0, has_side_effects=True),
-    )(positions, detuning.reshape(1, total), populations.reshape(1, width), section)
+    )(positions, detuning.reshape(1, total), populations.reshape(1, width), section.reshape(2 * cols, width))
     return (base + 0.5 * TIME_STEP * rate, accum + TIME_STEP / 3.0 * rate)
 
 

time: 9.28 us -> 9.06 us (0.976)
  Pallas kernels: 7.81 us -> 7.59 us
    pallas_call x1, Pallas kernels: 7.81 us -> 7.59 us  [local(): pl.pallas_call(functools.partial(kernel, n_row, n_grp), out_shape=pltpu.V...]
where the time goes in v2:
time: 9.06 us; the launch traced here: 8.89 us
  Pallas kernels  7.59 us (84%)
  between operations  0.67 us (7%)
  other arithmetic  0.62 us (7%)
    pallas_call x1, Pallas kernels, local(): pl.pallas_call(functools.partial(kernel, n_row, n_grp), out_shape=pltpu.V...  7.59 us
    add x1, other arithmetic, local(): return (base + 0.5 * TIME_STEP * rate, accum + TIME_STEP / 3.0 * rate)  0.62 us

profile of v2, /device:TPU:0, one launch (start us, length us, event | category | flops | bytes accessed | tf_op | source)
XLA Modules:
  0.0 8.9 jit_solution(17670019360468278216)
XLA Ops:
  0.6 0.0 copy-start
  0.6 0.0 copy-start.1
  0.7 7.6 %shard_map.77 = f32[2,16,128]{2,1,0:T(8,128)S(1)} custom-call(f32[3,1024]{1,0:T(4,128)} %pos_in.1, f32[1,1024]{1,0:T(1,128)} %bitcast.4, f32[1,128]{1,0:T(1,128)} %bitcast.5, f32[32,128]{1,0:T(8,128)} %bitcast.3), custom_call_target="tpu_custom_call" | custom-call | tf_op jit(solution)/shard_map/pallas_call | solution.py:393
  8.3 0.0 copy-done
  8.3 0.0 copy-done.1
  8.3 0.6 %multiply_add_fusion = (f32[2,16,128]{2,1,0:T(8,128)}, f32[2,16,128]{2,1,0:T(8,128)}) fusion(f32[2,16,128]{2,1,0:T(8,128)S(1)} %copy-done, f32[2,16,128]{2,1,0:T(8,128)S(1)} %shard_map.77, f32[2,16,128]{2,1,0:T(8,128)S(1)} %copy-done.1), kind=kLoop, calls=%fused_computation | loop fusion | flops 16384 | bytes 81920 | tf_op jit(solution)/shard_map/add | solution.py:416
Async XLA Ops:
  0.6 7.6 %copy-start = (f32[2,16,128]{2,1,0:T(8,128)S(1)}, f32[2,16,128]{2,1,0:T(8,128)}, u32[]{:S(2)}) copy-start(f32[2,16,128]{2,1,0:T(8,128)} %param.11) | copy-start | bytes 49156
  0.6 7.6 %copy-start.1 = (f32[2,16,128]{2,1,0:T(8,128)S(1)}, f32[2,16,128]{2,1,0:T(8,128)}, u32[]{:S(2)}) copy-start(f32[2,16,128]{2,1,0:T(8,128)} %param.9) | copy-start | bytes 49156

commit v3 on v2

--- a/solution.py
+++ b/solution.py
@@ -12,6 +12,7 @@
 PAD = 16
 TILE = 128
 AMPLITUDE = -0.75
+PAUSE = 1
 
 HALF_SIN = (4.442882834149929, -7.308241154546326, 3.606288958225646, -0.8457635961475002, 0.10920575363724722)
 HALF_COS = (1.4142134965650124, -6.97885098823893, 5.739461170681154, -1.8835629872981716, 0.31069819180355424)
@@ -78,6 +79,7 @@
     rhs_lo,
     row_buf,
     grp_buf,
+    coef,
     send_sem,
     row_recv,
     grp_recv,
@@ -86,6 +88,76 @@
     load_sem,
 ):
     cols, width = sec_in.shape[0] // 2, sec_in.shape[1]
+    me = lax.axis_index("row")
+    mine = lax.axis_index("grp")
+    slab = cols * n_grp
+    barrier = pltpu.get_barrier_semaphore()
+
+    last = n_row - 2
+    pair = me // 2
+    odd = lax.rem(me, 2)
+    partner = me + 1 - 2 * odd
+    in_first = me < 2
+    in_last = me >= last
+    between = jnp.logical_not(in_first | in_last)
+    even = odd == 0
+    low = jnp.minimum(mine, 1)
+    ahead = in_first & even & (mine > 0)
+    GO, LATE, WORD = 0, 1, 2
+    NEXT, REST = 0, 1
+
+    def to_row(sem, lo, hi):
+        def body(p, carry):
+            pl.semaphore_signal(sem, inc=1, device_id={"row": p}, device_id_type=MESH)
+            return carry
+
+        lax.fori_loop(lo, hi, body, 0)
+
+    def to_grp(sem, lo, hi):
+        def body(p, carry):
+            pl.semaphore_signal(sem, inc=1, device_id={"grp": p}, device_id_type=MESH)
+            return carry
+
+        lax.fori_loop(lo, hi, body, 0)
+
+    slab_part = stage.at[0 : 2 * cols]
+
+    def send_row(lo, hi):
+        def body(p, carry):
+            pltpu.make_async_remote_copy(
+                stage,
+                row_buf.at[me],
+                send_sem.at[0],
+                row_recv.at[me // last],
+                device_id={"row": p},
+                device_id_type=MESH,
+            ).start()
+            return carry
+
+        lax.fori_loop(lo, hi, body, 0)
+
+    def send_grp(lo, hi, source):
+        def body(p, carry):
+            pltpu.make_async_remote_copy(
+                source,
+                grp_buf.at[mine],
+                send_sem.at[1],
+                grp_recv.at[mine // (n_grp - 1)],
+                device_id={"grp": p},
+                device_id_type=MESH,
+            ).start()
+            return carry
+
+        lax.fori_loop(lo, hi, body, 0)
+
+    def arrived(part, sem):
+        pltpu.make_async_copy(part, part, sem).wait()
+
+    @pl.when(ahead)
+    def _():
+        pl.semaphore_wait(barrier, 1)
+        send_grp(0, 1, sec_in)
+
     section_loads = [
         pltpu.make_async_copy(src, dst, load_sem.at[0])
         for src, dst in (
@@ -97,68 +169,6 @@
     det_load = pltpu.make_async_copy(det_in, det_ref, load_sem.at[2])
     for load in (*section_loads, pos_load, det_load):
         load.start()
-    me = lax.axis_index("row")
-    mine = lax.axis_index("grp")
-    slab = cols * n_grp
-
-    barrier = pltpu.get_barrier_semaphore()
-
-    last = n_row - 2
-    pair = me // 2
-    odd = lax.rem(me, 2)
-    partner = me + 1 - 2 * odd
-    in_first = me < 2
-    in_last = me >= last
-    between = jnp.logical_not(in_first | in_last)
-    even = odd == 0
-    GO, LATE, WORD = 0, 1, 2
-
-    def to_row(sem, lo, hi):
-        def body(p, carry):
-            pl.semaphore_signal(sem, inc=1, device_id={"row": p}, device_id_type=MESH)
-            return carry
-
-        lax.fori_loop(lo, hi, body, 0)
-
-    def to_grp(sem, lo, hi):
-        def body(p, carry):
-            pl.semaphore_signal(sem, inc=1, device_id={"grp": p}, device_id_type=MESH)
-            return carry
-
-        lax.fori_loop(lo, hi, body, 0)
-
-    slab_part = stage.at[0 : 2 * cols]
-
-    def send_row(lo, hi):
-        def body(p, carry):
-            pltpu.make_async_remote_copy(
-                stage,
-                row_buf.at[me],
-                send_sem.at[0],
-                row_recv.at[me // last],
-                device_id={"row": p},
-                device_id_type=MESH,
-            ).start()
-            return carry
-
-        lax.fori_loop(lo, hi, body, 0)
-
-    def send_grp(lo, hi, source):
-        def body(p, carry):
-            pltpu.make_async_remote_copy(
-                source,
-                grp_buf.at[mine],
-                send_sem.at[1],
-                grp_recv,
-                device_id={"grp": p},
-                device_id_type=MESH,
-            ).start()
-            return carry
-
-        lax.fori_loop(lo, hi, body, 0)
-
-    def arrived(part, sem):
-        pltpu.make_async_copy(part, part, sem).wait()
 
     @pl.when(even & (mine > 0))
     def _():
@@ -180,16 +190,20 @@
     to_row(barrier, after, n_row)
 
     before = jnp.where(in_first, 0, jnp.where(in_last, last, 2))
-    low = jnp.minimum(mine, 1)
     met = before + jnp.where(even, low, 1 + mine + mine - low)
 
-    @pl.when(met > 0)
+    @pl.when((met > 0) & jnp.logical_not(ahead))
     def _():
         with jax.named_scope("bar"):
             pl.semaphore_wait(barrier, met)
 
-    send_grp(0, low, sec_in)
-    to_grp(grp_ready.at[mine - low], 0, low)
+    send_grp(0, jnp.where(even & jnp.logical_not(ahead), low, 0), sec_in)
+
+    def answer_lower(lo, hi):
+        to_grp(grp_ready.at[REST], lo, jnp.minimum(hi, mine - 1))
+        to_grp(grp_ready.at[NEXT], jnp.maximum(lo, mine - 1), hi)
+
+    answer_lower(0, low)
 
     @pl.when(between)
     def _():
@@ -202,7 +216,7 @@
     @pl.when(jnp.logical_not(even))
     def _():
         pl.semaphore_signal(row_ready.at[WORD], inc=1, device_id={"row": partner}, device_id_type=MESH)
-        to_grp(grp_ready.at[mine - low], low, mine)
+        answer_lower(low, mine)
 
     with jax.named_scope("load"):
         arrived(stage, load_sem.at[0])
@@ -212,9 +226,9 @@
     def _():
         with jax.named_scope("word"):
             pl.semaphore_wait(row_ready.at[WORD], 1)
-        to_grp(grp_ready.at[mine - low], low, mine)
-
-    send_grp(low, mine, slab_part)
+        answer_lower(low, mine)
+        send_grp(low, mine, slab_part)
+
     send_row(partner, partner + 1)
 
     with jax.named_scope("loadpos"):
@@ -255,29 +269,27 @@
         return lax.rem(first + j, total)
 
     with jax.named_scope("couple"):
-        spread(first, 0)
-        for j in range(tiles):
-            spread(tile_at(j + 1), (j + 1) % 2)
-            fill(tile_at(j), j % 2, sub_ids + j * TILE == lane_ids)
+        def lower_from_odd():
+            @pl.when(jnp.logical_not(even))
+            def _():
+                send_grp(0, mine, slab_part)
 
         def step(j, carry):
             spread(tile_at(j + 1), lax.rem(j + 1, 2))
             fill(tile_at(j), lax.rem(j, 2), None)
             return carry
 
-        UNROLL = 7 if (total - tiles) % 7 == 0 else 1
-        if UNROLL == total - tiles:
-            for j in range(tiles, total):
-                if j + 1 < total:
-                    spread(tile_at(j + 1), (j + 1) % 2)
-                fill(tile_at(j), j % 2, None)
-        else:
+        flat = total <= 16
+        spread(first, 0)
+        for j in range(total if flat else tiles):
+            if j == tiles + PAUSE:
+                lower_from_odd()
+            if j + 1 < total:
+                spread(tile_at(j + 1), (j + 1) % 2)
+            fill(tile_at(j), j % 2, sub_ids + j * TILE == lane_ids if j < tiles else None)
+        if not flat:
+            lower_from_odd()
             lax.fori_loop(tiles, total, step, 0)
-
-    def answer_grp(p, carry):
-        pl.semaphore_wait(grp_ready.at[p - 1], 1)
-        send_grp(p, p + 1, slab_part)
-        return carry
 
     @pl.when(in_first & (last > 2))
     def _():
@@ -297,8 +309,11 @@
         send_row(2, 2 * pair)
         send_row(2 * pair + 2, last)
 
-    with jax.named_scope("ansgrp1"):
-        lax.fori_loop(mine + 1, jnp.minimum(mine + 2, n_grp), answer_grp, 0)
+    @pl.when(mine < n_grp - 1)
+    def _():
+        with jax.named_scope("ansnext"):
+            pl.semaphore_wait(grp_ready.at[NEXT], 1)
+        send_grp(mine + 1, mine + 2, slab_part)
 
     @pl.when(jnp.logical_not(in_last))
     def _():
@@ -306,8 +321,11 @@
             pl.semaphore_wait(row_ready.at[LATE], 2)
         send_row(last, n_row)
 
-    with jax.named_scope("ansgrp2"):
-        lax.fori_loop(mine + 2, n_grp, answer_grp, 0)
+    @pl.when(mine < n_grp - 2)
+    def _():
+        with jax.named_scope("ansrest"):
+            pl.semaphore_wait(grp_ready.at[REST], n_grp - 2 - mine)
+        send_grp(mine + 2, n_grp, slab_part)
 
     col_start = pl.multiple_of(mine * cols, cols)
     eye = lax.broadcasted_iota(jnp.int32, (cols, TILE), 0) + col_start == lax.broadcasted_iota(
@@ -320,7 +338,11 @@
     w_real, w_imag = coupling(own_cols, slab_rows, eye)
     w_real = AMPLITUDE * w_real + jnp.where(eye, det_ref[:, :TILE], 0.0)
     w_imag = AMPLITUDE * w_imag + jnp.where(eye, -0.5, 0.0)
-    l_hi, l_lo = split(jnp.concatenate([w_real, w_imag], axis=0)[:, :slab])
+    most = slab - cols
+    l_hi, l_lo = split(jnp.concatenate([w_real, w_imag], axis=0)[:, :most])
+    for j in range(cols):
+        for lead, w in ((0, w_real), (cols, w_imag)):
+            coef[j, lead : lead + cols] = jnp.broadcast_to(w[:, most + j : most + j + 1], (cols, width))
 
     y_local = stage[0 : 2 * cols]
     row_buf[me] = stage[...]
@@ -362,21 +384,56 @@
     z_imag = z[:cols, width:] + z[cols : 2 * cols, :width]
     shift = z[2 * cols : 2 * cols + 1, :width]
 
-    with jax.named_scope("wgrp"):
-        arrived(grp_buf.at[0 : n_grp - 1], grp_recv)
-    blocks = [grp_buf[g] for g in range(n_grp)]
+    y_real, y_imag = y_local[:cols], y_local[cols:]
+    total_shift = shift + det_ref[:, pl.ds(my_start, width)]
+    z_real = z_real + total_shift * y_real + 0.5 * y_imag
+    z_imag = z_imag + total_shift * y_imag - 0.5 * y_real
+
+    top = n_grp - 1
+    if n_grp > 2:
+        with jax.named_scope("wgrp"):
+
+            @pl.when(mine < top)
+            def _():
+                arrived(grp_buf.at[0 : top - 1], grp_recv.at[0])
+
+            @pl.when(mine == top)
+            def _():
+                arrived(grp_buf.at[0:top], grp_recv.at[0])
+
+    elif n_grp == 2:
+
+        @pl.when(mine == top)
+        def _():
+            arrived(grp_buf.at[0:top], grp_recv.at[0])
+
+    blocks = [grp_buf[g] for g in range(top)]
     full = jnp.concatenate(
         [jnp.concatenate([block[:cols], block[cols:]], axis=1) for block in blocks], axis=0
     )
     f_hi, f_lo = split(full)
     v = bdot(l_hi, f_hi) + bdot(l_lo, f_hi) + bdot(l_hi, f_lo)
-    v_real = v[:cols, :width] + v[cols:, width:]
-    v_imag = v[:cols, width:] - v[cols:, :width]
-
-    y_real, y_imag = y_local[:cols], y_local[cols:]
-    total_shift = shift + det_ref[:, pl.ds(my_start, width)]
-    z_real = z_real + total_shift * y_real + 0.5 * y_imag
-    z_imag = z_imag + total_shift * y_imag - 0.5 * y_real
+    z_imag = z_imag - (v[:cols, width:] - v[cols:, :width])
+    z_real = z_real - (v[:cols, :width] + v[cols:, width:])
+
+    with jax.named_scope("wtop"):
+
+        @pl.when(mine < top)
+        def _():
+            arrived(grp_buf.at[0], grp_recv.at[1])
+
+    sums = [[jnp.zeros((cols, width), jnp.float32)] * 4 for _ in range(2)]
+    for j in range(cols):
+        fr = grp_buf[top, j : j + 1]
+        fi = grp_buf[top, cols + j : cols + j + 1]
+        wr, wi = coef[j, :cols], coef[j, cols:]
+        k = 2 * (j % 2)
+        sums[0][k] = sums[0][k] + wr * fr
+        sums[0][k + 1] = sums[0][k + 1] + wi * fi
+        sums[1][k] = sums[1][k] + wr * fi
+        sums[1][k + 1] = sums[1][k + 1] + wi * fr
+    v_real = (sums[0][0] + sums[0][1]) + (sums[0][2] + sums[0][3])
+    v_imag = (sums[1][0] + sums[1][2]) - (sums[1][1] + sums[1][3])
     out_ref[0] = z_imag - v_imag
     out_ref[1] = v_real - z_real
 
@@ -404,11 +461,12 @@
             pltpu.VMEM((total, 2 * width), jnp.bfloat16),
             pltpu.VMEM((n_row, 2 * cols + 1, width), jnp.float32),
             pltpu.VMEM((n_grp, 2 * cols, width), jnp.float32),
+            pltpu.VMEM((cols, 2 * cols, width), jnp.float32),
             pltpu.SemaphoreType.DMA((2,)),
             pltpu.SemaphoreType.DMA((2,)),
-            pltpu.SemaphoreType.DMA(()),
+            pltpu.SemaphoreType.DMA((2,)),
             pltpu.SemaphoreType.REGULAR((3,)),
-            pltpu.SemaphoreType.REGULAR((n_grp - 1,)),
+            pltpu.SemaphoreType.REGULAR((2,)),
             pltpu.SemaphoreType.DMA((3,)),
         ],
         compiler_params=pltpu.CompilerParams(collective_id=0, has_side_effects=True),

time: 9.06 us -> 8.76 us (0.967)
  Pallas kernels: 7.59 us -> 7.29 us
    pallas_call x1, Pallas kernels: 7.59 us -> 7.29 us  [local(): pl.pallas_call(functools.partial(kernel, n_row, n_grp), out_shape=pltpu.V...]
where the time goes in v3:
time: 8.76 us; the launch traced here: 8.59 us
  Pallas kernels  7.29 us (83%)
  between operations  0.67 us (8%)
  other arithmetic  0.62 us (7%)
    pallas_call x1, Pallas kernels, local(): pl.pallas_call(functools.partial(kernel, n_row, n_grp), out_shape=pltpu.V...  7.29 us
    add x1, other arithmetic, local(): return (base + 0.5 * TIME_STEP * rate, accum + TIME_STEP / 3.0 * rate)  0.62 us

profile of v3, /device:TPU:0, one launch (start us, length us, event | category | flops | bytes accessed | tf_op | source)
XLA Modules:
  0.0 8.6 jit_solution(13698366217978071777)
XLA Ops:
  0.6 0.0 copy-start
  0.6 0.0 copy-start.1
  0.7 7.3 %shard_map.77 = f32[2,16,128]{2,1,0:T(8,128)S(1)} custom-call(f32[3,1024]{1,0:T(4,128)} %pos_in.1, f32[1,1024]{1,0:T(1,128)} %bitcast.4, f32[1,128]{1,0:T(1,128)} %bitcast.5, f32[32,128]{1,0:T(8,128)} %bitcast.3), custom_call_target="tpu_custom_call" | custom-call | tf_op jit(solution)/shard_map/pallas_call | solution.py:450
  7.9 0.0 copy-done
  8.0 0.0 copy-done.1
  8.0 0.6 %multiply_add_fusion = (f32[2,16,128]{2,1,0:T(8,128)}, f32[2,16,128]{2,1,0:T(8,128)}) fusion(f32[2,16,128]{2,1,0:T(8,128)S(1)} %copy-done, f32[2,16,128]{2,1,0:T(8,128)S(1)} %shard_map.77, f32[2,16,128]{2,1,0:T(8,128)S(1)} %copy-done.1), kind=kLoop, calls=%fused_computation | loop fusion | flops 16384 | bytes 81920 | tf_op jit(solution)/shard_map/add | solution.py:474
Async XLA Ops:
  0.6 7.3 %copy-start = (f32[2,16,128]{2,1,0:T(8,128)S(1)}, f32[2,16,128]{2,1,0:T(8,128)}, u32[]{:S(2)}) copy-start(f32[2,16,128]{2,1,0:T(8,128)} %param.11) | copy-start | bytes 49156
  0.6 7.3 %copy-start.1 = (f32[2,16,128]{2,1,0:T(8,128)S(1)}, f32[2,16,128]{2,1,0:T(8,128)}, u32[]{:S(2)}) copy-start(f32[2,16,128]{2,1,0:T(8,128)} %param.9) | copy-start | bytes 49156
